TPU v7x, 32 devices: a whole 2x2x4 slice. The times are simulated.
32 devices in a mesh: band: 8 (over z, y), grid: 4 (over x, core).
Axes of the slice: x: 2, y: 2, z: 4, core: 2. Of those that a mesh axis runs over, the one named last changes fastest.
Arguments:
- orbitals: bfloat16 [8, 128, 128, 128], P('band', 'grid'), may hold values from -3 to 3
- trial_vectors: bfloat16 [2, 8, 128, 128, 128], P(None, 'band', 'grid'), may hold values from -6 to 6
- alda_kernel: float32 [128, 128, 128], P('grid'), may hold values from -2 to -0.5
- local_potential: float32 [128, 128, 128], P('grid'), may hold values from -2 to 1
- band_energies: float32 [8], P('band'), may hold values from -1.5 to -0.2
Outputs:
- sigma_real: float32 [2, 8, 128, 128, 128], P(None, 'band', 'grid')
- sigma_imag: float32 [2, 8, 128, 128, 128], P(None, 'band', 'grid')
All inputs are finite; a program needn't handle non-finite values.
Results may differ from a plain program's by a relative error of at most 0.0003.
Values sent between devices are 32-bit elements; how exact they have to be, the bound alone decides.
A program may use at most 64 MiB of HBM per device.

v0:
```python
import math
import jax
import jax.numpy as jnp
from jax import lax
from jax.sharding import PartitionSpec as P

box_length = 30.0
highest = lax.Precision.HIGHEST


def tables(length):
    positions = jnp.arange(length, dtype=jnp.int32)
    wrapped = positions[:, None] * positions[None, :] % length
    angles = wrapped.astype(jnp.float32) * (2.0 * math.pi / length)
    return (jnp.cos(angles), jnp.sin(angles))


def contract(pattern, left_operand, right_operand):
    return jnp.einsum(pattern, left_operand, right_operand, precision=highest)


def rotate(pattern, real_part, imag_part, cosine_table, sine_table, orient):
    new_real = contract(pattern, real_part, cosine_table) - orient * contract(
        pattern, imag_part, sine_table
    )
    new_imag = contract(pattern, imag_part, cosine_table) + orient * contract(
        pattern, real_part, sine_table
    )
    return (new_real, new_imag)


def rotate_real(pattern, real_part, cosine_table, sine_table, orient):
    return (
        contract(pattern, real_part, cosine_table),
        orient * contract(pattern, real_part, sine_table),
    )


def frequency(length, offset, extent):
    positions = offset + jnp.arange(extent, dtype=jnp.int32)
    signed = jnp.where(2 * positions < length, positions, positions - length)
    return signed.astype(jnp.float32)


def coulomb(first_freq, second_freq, third_freq):
    squared = (
        first_freq[:, None, None] ** 2
        + second_freq[None, :, None] ** 2
        + third_freq[None, None, :] ** 2
    )
    scaled = box_length**2 / math.pi / jnp.maximum(squared, 1.0)
    return jnp.where(squared > 0, scaled, 0.0)


def potential_split(density_share, cosine_table, sine_table, length):
    real_part, imag_part = rotate_real(
        "kxyz,zg->kxgy", density_share, cosine_table, sine_table, -1.0
    )
    arrived = lax.all_to_all(
        jnp.stack((real_part, imag_part)), "band", split_axis=3, concat_axis=4, tiled=True
    )
    real_part, imag_part = rotate(
        "kxzy,yg->kgzx", arrived[0], arrived[1], cosine_table, sine_table, -1.0
    )
    arrived = lax.all_to_all(
        jnp.stack((real_part, imag_part)), "grid", split_axis=2, concat_axis=4, tiled=True
    )
    real_part, imag_part = rotate(
        "kyzx,xg->kyzg", arrived[0], arrived[1], cosine_table, sine_table, -1.0
    )
    rows_here = real_part.shape[1]
    planes_here = real_part.shape[2]
    kernel = coulomb(
        frequency(length, lax.axis_index("grid") * rows_here, rows_here),
        frequency(length, lax.axis_index("band") * planes_here, planes_here),
        frequency(length, 0, length),
    )
    real_part = real_part * kernel[None]
    imag_part = imag_part * kernel[None]
    real_part, imag_part = rotate(
        "kyzg,gx->kyzx", real_part, imag_part, cosine_table, sine_table, 1.0
    )
    arrived = lax.all_to_all(
        jnp.stack((real_part, imag_part)), "grid", split_axis=4, concat_axis=2, tiled=True
    )
    real_part, imag_part = rotate(
        "kgzx,gy->kxzy", arrived[0], arrived[1], cosine_table, sine_table, 1.0
    )
    arrived = lax.all_to_all(
        jnp.stack((real_part, imag_part)), "band", split_axis=4, concat_axis=3, tiled=True
    )
    restored = contract("kxgy,gz->kxyz", arrived[0], cosine_table) - contract(
        "kxgy,gz->kxyz", arrived[1], sine_table
    )
    return restored / float(length**3)


def per_device(orbitals, trial_vectors, alda_kernel, local_potential, band_energies):
    length = orbitals.shape[2]
    cosine_table, sine_table = tables(length)
    orbital_wide = orbitals.astype(jnp.float32)
    trial_wide = trial_vectors.astype(jnp.float32)
    partial_value = 2.0 * jnp.sum(trial_wide * orbital_wide[None], axis=1)
    density_share = lax.psum_scatter(partial_value, "band", scatter_dimension=2, tiled=True)
    row_count = density_share.shape[2]
    kernel_rows = lax.dynamic_slice_in_dim(
        alda_kernel, lax.axis_index("band") * row_count, row_count, 1
    )
    hartree = potential_split(density_share, cosine_table, sine_table, length)
    potential = lax.all_gather(
        hartree + kernel_rows[None] * density_share, "band", axis=2, tiled=True
    )
    weight = local_potential[None] - band_energies[:, None, None, None]
    fields = potential[:, None] * orbital_wide[None] + weight[None] * trial_wide
    trial_count = trial_vectors.shape[0]
    norm_factor = float(length) ** (-1.5)
    pieces = []
    for trial_index in range(trial_count):
        real_part, imag_part = rotate_real(
            "mxyz,zg->mxyg", fields[trial_index], cosine_table, sine_table, -1.0
        )
        real_part, imag_part = rotate(
            "mxyz,yg->mgzx", real_part, imag_part, cosine_table, sine_table, -1.0
        )
        received = lax.all_to_all(
            jnp.stack((real_part, imag_part)), "grid", split_axis=2, concat_axis=4, tiled=True
        )
        finish_real_part, finish_imag_part = rotate(
            "myzx,xg->myzg", received[0], received[1], cosine_table, sine_table, -1.0
        )
        pieces.append(jnp.stack((finish_real_part * norm_factor, finish_imag_part * norm_factor)))
    results = jnp.stack(pieces, axis=1)
    return (results[0], results[1])


def solution(mesh):
    placed = (
        P("band", "grid", None, None),
        P(None, "band", "grid", None, None),
        P("grid", None, None),
        P("grid", None, None),
        P("band"),
    )
    return jax.shard_map(
        per_device,
        mesh=mesh,
        in_specs=placed,
        out_specs=(P(None, "band", "grid", None, None), P(None, "band", "grid", None, None)),
        check_vma=False,
    )
```

profile of v0, /device:TPU:0, one launch (start us, length us, event | category | flops | bytes accessed | tf_op | source)
XLA Modules:
  0.0 582.9 jit_solution(3529673383581125716)
XLA Ops:
  13.0 91.5 %reduce-scatter.2.cloned.1.call-done = f32[2,32,16,128]{3,2,1,0:T(8,128)} async-done(((f32[2,32,128,128]{3,2,1,0:T(8,128)}), f32[2,32,16,128]{3,2,1,0:T(8,128)}) %reduce-scatter.2.cloned.1.call-update) | async-done | bytes 524304 | tf_op jit(solution)/shard_map/reduce_scatter | solution.py:104
  108.4 4.4 copy.166
  112.8 4.8 reshape.245
  117.6 4.6 all-to-all-start
  122.2 25.6 %all-to-all-done = f32[8,1,32768]{2,1,0:T(1,128)S(1)} async-done(((f32[8,1,32768]{2,1,0:T(1,128)}), f32[8,1,32768]{2,1,0:T(1,128)S(1)}, u32[]{:S(2)}, u32[]{:S(2)}) %all-to-all-start) | async-done | bytes 1048608 | tf_op jit(solution)/shard_map/all_to_all | solution.py:59
  149.4 4.3 reduce
  167.6 14.0 %fusion.27 = f32[1,2,128,16,32]{2,4,3,1,0:T(8,128)S(1)} fusion(f32[128,2,32,16]{0,2,3,1:T(8,128)S(1)} %convolution_multiply_fusion.1, f32[2,32,16,128]{1,3,2,0:T(8,128)S(1)} %bitcast.275), kind=kOutput, calls=%fused_computation.44 | convolution fusion | flops 201687040 | bytes 1572864 | tf_op jit(solution)/shard_map/kxzy,yg->kgzx/dot_general | solution.py:19
  185.1 4.4 copy.174
  189.5 4.8 reshape.247
  194.4 4.2 all-to-all-start.1
  198.9 14.2 %all-to-all-done.1 = f32[4,1,65536]{2,1,0:T(1,128)} async-done(((f32[4,1,65536]{2,1,0:T(1,128)}), f32[4,1,65536]{2,1,0:T(1,128)}, u32[]{:S(2)}, u32[]{:S(2)}) %all-to-all-start.1) | async-done | bytes 1048608 | tf_op jit(solution)/shard_map/all_to_all | solution.py:65
  213.1 4.6 reduce.1
  221.2 4.9 copy.248
  240.4 4.4 copy.176
  248.7 17.7 %all_to_all.90 = f32[4,1,65536]{2,1,0:T(1,128)} all-to-all(f32[4,1,65536]{2,1,0:T(1,128)S(1)} %reshape.249), channel_id=1, replica_groups=mesh['band'=8,'grid'=4] {'grid'}, dimensions={0} | all-to-all | bytes 2097152 | tf_op jit(solution)/shard_map/all_to_all | solution.py:83
  266.4 4.6 reduce.2
  274.5 4.9 copy.247
  290.9 4.4 copy.178
  295.3 4.8 reshape.251
  304.3 25.1 %all-to-all-done.3 = f32[8,1,32768]{2,1,0:T(1,128)S(1)} async-done(((f32[8,1,32768]{2,1,0:T(1,128)}), f32[8,1,32768]{2,1,0:T(1,128)S(1)}, u32[]{:S(2)}, u32[]{:S(2)}) %all-to-all-start.3) | async-done | bytes 1048608 | tf_op jit(solution)/shard_map/all_to_all | solution.py:89
  335.9 4.6 copy.179
  354.4 69.1 %all-gather.2.cloned.1.call-done = f32[2,32,128,128]{3,2,1,0:T(8,128)} async-done(((f32[2,32,16,128]{3,2,1,0:T(8,128)}), f32[2,32,128,128]{3,2,1,0:T(8,128)}) %all-gather.2.cloned.1.call-update) | async-done | bytes 4194320 | tf_op jit(solution)/shard_map/all_gather | solution.py:110
  423.5 4.7 fusion.2
  442.3 4.4 copy.188
  446.7 4.8 all-to-all-start.4
  467.1 4.4 copy.201
  471.6 28.2 %all-to-all-done.4 = f32[2,1,128,128,32]{3,4,1,0,2:T(8,128)} async-done(((f32[2,1,128,128,32]{3,4,1,0,2:T(8,128)}), f32[2,1,128,128,32]{3,4,1,0,2:T(8,128)}, u32[]{:S(2)}, u32[]{:S(2)}) %all-to-all-start.4) | async-done | bytes 4194336 | tf_op jit(solution)/shard_map/all_to_all | solution.py:125
  499.8 4.9 all-to-all-start.5
  511.9 5.0 multiply_bitcast_fusion.3
  517.0 4.0 fusion.90
  521.0 4.9 multiply_bitcast_fusion.2
  525.9 26.9 %all-to-all-done.5 = f32[2,1,128,128,32]{3,4,1,0,2:T(8,128)} async-done(((f32[2,1,128,128,32]{3,4,1,0,2:T(8,128)}), f32[2,1,128,128,32]{3,4,1,0,2:T(8,128)}, u32[]{:S(2)}, u32[]{:S(2)}) %all-to-all-start.5) | async-done | bytes 4194336 | tf_op jit(solution)/shard_map/all_to_all | solution.py:125
  (114 shorter events, 148.7 us)
Async XLA Ops:
  7.2 297.1 %copy-start = (f32[32,128,128]{2,1,0:T(8,128)S(1)}, f32[32,128,128]{2,1,0:T(8,128)}, u32[]{:S(2)}) copy-start(f32[32,128,128]{2,1,0:T(8,128)} %param.7) | copy-start | bytes 6291460
  7.2 97.3 %reduce-scatter.2.cloned.1.call-start = ((), (), s32[]{:S(2)}) async-start(), calls=%async_computation.7 | async-start | bytes 4718592 | tf_op jit(solution)/shard_map/reduce_scatter | solution.py:104
  7.2 3.0 copy-start.6
  8.9 1.4 copy-start.4
  117.6 30.2 %all-to-all-start = ((f32[8,1,32768]{2,1,0:T(1,128)}), f32[8,1,32768]{2,1,0:T(1,128)S(1)}, u32[]{:S(2)}, u32[]{:S(2)}) async-start(f32[8,1,32768]{2,1,0:T(1,128)} %reshape.245), calls=%async_computation.1 | async-start | bytes 2097152 | tf_op jit(solution)/shard_map/all_to_all | solution.py:59
  147.9 1.0 copy-start.10
  194.4 18.7 %all-to-all-start.1 = ((f32[4,1,65536]{2,1,0:T(1,128)}), f32[4,1,65536]{2,1,0:T(1,128)}, u32[]{:S(2)}, u32[]{:S(2)}) async-start(f32[4,1,65536]{2,1,0:T(1,128)} %reshape.247), calls=%async_computation.2 | async-start | bytes 2097152 | tf_op jit(solution)/shard_map/all_to_all | solution.py:65
  289.0 1.7 copy-start.11
  300.2 29.2 %all-to-all-start.3 = ((f32[8,1,32768]{2,1,0:T(1,128)}), f32[8,1,32768]{2,1,0:T(1,128)S(1)}, u32[]{:S(2)}, u32[]{:S(2)}) async-start(f32[8,1,32768]{2,1,0:T(1,128)} %reshape.251), calls=%async_computation.4 | async-start | bytes 2097152 | tf_op jit(solution)/shard_map/all_to_all | solution.py:89
  303.8 119.7 %all-gather.2.cloned.1.call-start = ((), (), s32[]{:S(2)}) async-start(), calls=%async_computation.8 | async-start | bytes 4718592 | tf_op jit(solution)/shard_map/all_gather | solution.py:110
  346.0 1.7 copy-start.9
  351.1 72.4 %copy-start.5 = (f32[32,128,128]{2,1,0:T(8,128)S(1)}, f32[32,128,128]{2,1,0:T(8,128)}, u32[]{:S(2)}) copy-start(f32[32,128,128]{2,1,0:T(8,128)} %copy-done.4) | copy-start | bytes 6291460
  428.2 2.1 copy-start.2
  446.7 53.1 %all-to-all-start.4 = ((f32[2,1,128,128,32]{3,4,1,0,2:T(8,128)}), f32[2,1,128,128,32]{3,4,1,0,2:T(8,128)}, u32[]{:S(2)}, u32[]{:S(2)}) async-start(f32[2,1,128,128,32]{3,4,1,0,2:T(8,128)} %copy.188), calls=%async_computation.5 | async-start | bytes 8388608 | tf_op jit(solution)/shard_map/all_to_all | solution.py:125
  451.6 3.8 copy-start.3
  499.8 53.1 %all-to-all-start.5 = ((f32[2,1,128,128,32]{3,4,1,0,2:T(8,128)}), f32[2,1,128,128,32]{3,4,1,0,2:T(8,128)}, u32[]{:S(2)}, u32[]{:S(2)}) async-start(f32[2,1,128,128,32]{3,4,1,0,2:T(8,128)} %copy.201), calls=%async_computation.6 | async-start | bytes 8388608 | tf_op jit(solution)/shard_map/all_to_all | solution.py:125
  567.6 3.6 copy-start.7
  567.6 3.6 copy-start.8
  572.2 3.6 copy-start.1
Sparse Core Ops, SparseCore 0:
  13.1 91.3 reduce-scatter.1
  350.5 72.9 all-gather.1
where the time goes:
time: 588 us; the launch traced here: 583 us
  waiting for transfers between devices  281 us (48%)
  local copies, waits for them, and re-layouts  108 us (18%)
  matrix products  103 us (18%)
  other arithmetic  35.2 us (6%)
  starting transfers between devices  22.7 us (4%)
  blocking collectives  17.7 us (3%)
  between operations  15.6 us (3%)
    dot_general x36, matrix products, contract(): return jnp.einsum(pattern, left_operand, right_operand, precision=highest)  99 us
    reduce_scatter x1, waiting for transfers between devices, per_device(): lax.psum_scatter(partial_value, 'band', scatter_dimension=2, tiled=True)  91.5 us
    all_gather x1, waiting for transfers between devices, per_device(): lax.all_gather(hartree + kernel_rows[None] * density_share, 'band', axis=...  69.1 us
    all_to_all x2, waiting for transfers between devices, per_device(): lax.all_to_all(jnp.stack((real_part, imag_part)), 'grid', split_axis=2, c...  55.1 us
    unnamed x32, local copies, waits for them, and re-layouts  34.5 us
    all_to_all x1, waiting for transfers between devices, potential_split(): lax.all_to_all(jnp.stack((real_part, imag_part)), 'band', split_axis=3, c...  25.6 us
    all_to_all x1, waiting for transfers between devices, potential_split(): lax.all_to_all(jnp.stack((real_part, imag_part)), 'band', split_axis=4, c...  25.1 us
    all_to_all x1, blocking collectives, potential_split(): lax.all_to_all(jnp.stack((real_part, imag_part)), 'grid', split_axis=4, c...  17.7 us
  transfers between devices with their start and end apart: 7, of which 7 were waited for; matrix products, arithmetic and copies ran while one was open for 8% of the time, Pallas kernels for 0%

commit v1 on v0

--- a/solution.py
+++ b/solution.py
@@ -6,6 +6,17 @@
 
 box_length = 30.0
 highest = lax.Precision.HIGHEST
+
+
+def in_blocks(value, dim, length):
+    before, after = (value.shape[:dim], value.shape[dim + 1 :])
+    return jnp.moveaxis(value.reshape(*before, length, -1, *after), dim, 0)
+
+
+def in_order(pieces, dim):
+    pieces = jnp.moveaxis(pieces, 0, dim)
+    shape = pieces.shape
+    return pieces.reshape(*shape[:dim], shape[dim] * shape[dim + 1], *shape[dim + 2 :])
 
 
 def tables(length):
@@ -86,9 +97,16 @@
     real_part, imag_part = rotate(
         "kgzx,gy->kxzy", arrived[0], arrived[1], cosine_table, sine_table, 1.0
     )
-    arrived = lax.all_to_all(
-        jnp.stack((real_part, imag_part)), "band", split_axis=4, concat_axis=3, tiled=True
-    )
+    x = jnp.stack((real_part, imag_part))
+    count, index = (lax.axis_size("band"), lax.axis_index("band"))
+    blocks = in_blocks(x, 4, count)
+    result = blocks
+    for step in range(1, count):
+        target, source = ((index + step) % count, (index - step) % count)
+        sent = lax.dynamic_index_in_dim(blocks, target, 0)
+        other = lax.ppermute(sent, "band", [(i, (i + step) % count) for i in range(count)])
+        result = lax.dynamic_update_slice_in_dim(result, other, source, axis=0)
+    arrived = in_order(result, 3)
     restored = contract("kxgy,gz->kxyz", arrived[0], cosine_table) - contract(
         "kxgy,gz->kxyz", arrived[1], sine_table
     )

time: 588 us -> 638 us (1.085)
  waiting for transfers between devices: 281 us -> 332 us
  starting transfers between devices: 22.7 us -> 51.7 us
  blocking collectives: 17.7 us -> 0 us
  local copies, waits for them, and re-layouts: 108 us -> 91.5 us
    ppermute x0 -> x7, waiting for transfers between devices: none -> 43.4 us  [potential_split(): lax.ppermute(sent, 'band', [(i, (i + step) % count) for i in range(count)])]
    ppermute x0 -> x7, starting transfers between devices: none -> 29 us  [potential_split(): lax.ppermute(sent, 'band', [(i, (i + step) % count) for i in range(count)])]
    all_gather x1, waiting for transfers between devices: 69.1 us -> 89 us  [per_device(): lax.all_gather(hartree + kernel_rows[None] * density_share, 'band', axis=...]
    all_to_all x1 -> x0, blocking collectives: 17.7 us -> none  [potential_split(): lax.all_to_all(jnp.stack((real_part, imag_part)), 'grid', split_axis=4, c...]
    all_to_all x1, waiting for transfers between devices: 25.1 us -> 13.7 us  [potential_split(): lax.all_to_all(jnp.stack((real_part, imag_part)), 'grid', split_axis=4, c...]
    unnamed x32, local copies, waits for them, and re-layouts: 34.5 us -> 27.3 us
    another operation x4 -> x3, local copies, waits for them, and re-layouts: 17.6 us -> 13.2 us  [potential_split(): jnp.stack((real_part, imag_part))]
  transfers between devices with their start and end apart: 7 -> 14, of which waited for: 7 -> 11; matrix products, arithmetic and copies ran while one was open for 8% -> 7% of each run, Pallas kernels for 0% -> 0%
where the time goes in v1:
time: 638 us; the launch traced here: 633 us
  waiting for transfers between devices  332 us (52%)
  matrix products  107 us (17%)
  local copies, waits for them, and re-layouts  91.5 us (14%)
  starting transfers between devices  51.7 us (8%)
  other arithmetic  34.3 us (5%)
  between operations  16 us (3%)
    dot_general x36, matrix products, contract(): return jnp.einsum(pattern, left_operand, right_operand, precision=highest)  102 us
    reduce_scatter x1, waiting for transfers between devices, per_device(): lax.psum_scatter(partial_value, 'band', scatter_dimension=2, tiled=True)  91.5 us
    all_gather x1, waiting for transfers between devices, per_device(): lax.all_gather(hartree + kernel_rows[None] * density_share, 'band', axis=...  89 us
    all_to_all x2, waiting for transfers between devices, per_device(): lax.all_to_all(jnp.stack((real_part, imag_part)), 'grid', split_axis=2, c...  55 us
    ppermute x7, waiting for transfers between devices, potential_split(): lax.ppermute(sent, 'band', [(i, (i + step) % count) for i in range(count)])  43.4 us
    ppermute x7, starting transfers between devices, potential_split(): lax.ppermute(sent, 'band', [(i, (i + step) % count) for i in range(count)])  29 us
    unnamed x32, local copies, waits for them, and re-layouts  27.3 us
    all_to_all x1, waiting for transfers between devices, potential_split(): lax.all_to_all(jnp.stack((real_part, imag_part)), 'band', split_axis=3, c...  25.6 us
  transfers between devices with their start and end apart: 14, of which 11 were waited for; matrix products, arithmetic and copies ran while one was open for 7% of the time, Pallas kernels for 0%

profile of v1, /device:TPU:0, one launch (start us, length us, event | category | flops | bytes accessed | tf_op | source)
XLA Modules:
  0.0 633.0 jit_solution(13604545400056861993)
XLA Ops:
  13.0 91.5 %reduce-scatter.2.cloned.1.call-done = f32[2,32,16,128]{3,2,1,0:T(8,128)} async-done(((f32[2,32,128,128]{3,2,1,0:T(8,128)}), f32[2,32,16,128]{3,2,1,0:T(8,128)}) %reduce-scatter.2.cloned.1.call-update) | async-done | bytes 524304 | tf_op jit(solution)/shard_map/reduce_scatter | solution.py:122
  108.4 4.4 copy.167
  112.8 4.8 reshape.258
  117.6 4.6 all-to-all-start
  122.3 25.6 %all-to-all-done = f32[8,1,32768]{2,1,0:T(1,128)S(1)} async-done(((f32[8,1,32768]{2,1,0:T(1,128)}), f32[8,1,32768]{2,1,0:T(1,128)S(1)}, u32[]{:S(2)}, u32[]{:S(2)}) %all-to-all-start) | async-done | bytes 1048608 | tf_op jit(solution)/shard_map/all_to_all | solution.py:70
  149.4 4.3 reduce
  167.6 14.5 %fusion.28 = f32[1,2,128,16,32]{2,4,3,1,0:T(8,128)S(1)} fusion(f32[128,2,32,16]{0,2,3,1:T(8,128)S(1)} %convolution_multiply_fusion.1, f32[2,32,16,128]{1,3,2,0:T(8,128)S(1)} %bitcast.291), kind=kOutput, calls=%fused_computation.60 | convolution fusion | flops 201687040 | bytes 1572864 | tf_op jit(solution)/shard_map/kxzy,yg->kgzx/dot_general | solution.py:30
  185.7 4.4 copy.175
  190.1 4.8 reshape.260
  194.9 4.2 all-to-all-start.1
  199.5 14.2 %all-to-all-done.1 = f32[4,1,65536]{2,1,0:T(1,128)} async-done(((f32[4,1,65536]{2,1,0:T(1,128)}), f32[4,1,65536]{2,1,0:T(1,128)}, u32[]{:S(2)}, u32[]{:S(2)}) %all-to-all-start.1) | async-done | bytes 1048608 | tf_op jit(solution)/shard_map/all_to_all | solution.py:76
  213.7 4.6 reduce.1
  221.7 4.9 copy.249
  242.5 4.4 copy.177
  246.9 4.8 reshape.262
  256.0 13.7 %all-to-all-done.2 = f32[4,1,65536]{2,1,0:T(1,128)S(1)} async-done(((f32[4,1,65536]{2,1,0:T(1,128)}), f32[4,1,65536]{2,1,0:T(1,128)S(1)}, u32[]{:S(2)}, u32[]{:S(2)}) %all-to-all-start.2) | async-done | bytes 1048608 | tf_op jit(solution)/shard_map/all_to_all | solution.py:94
  276.8 4.9 copy.248
  299.3 3.9 collective-permute-start.5
  305.3 9.7 %collective-permute-done = f32[1,2,2,32,16,16]{3,5,0,4,2,1:T(8,128)S(1)} collective-permute-done((f32[1,2,2,32,16,16]{3,5,0,4,2,1:T(8,128)S(1)}, f32[1,2,2,32,16,16]{3,5,0,4,2,1:T(8,128)S(1)}, u32[]{:S(2)}, u32[]{:S(2)}) %collective-permute-start) | collective-permute-done | bytes 131104 | tf_op jit(solution)/shard_map/ppermute | solution.py:107
  315.8 21.5 %collective-permute-start.6 = (f32[1,2,2,32,16,16]{3,5,0,4,2,1:T(8,128)S(1)}, f32[1,2,2,32,16,16]{3,5,0,4,2,1:T(8,128)S(1)}, u32[]{:S(2)}, u32[]{:S(2)}) collective-permute-start(f32[1,2,2,32,16,16]{3,5,0,4,2,1:T(8,128)S(1)} %get-tuple-element.20), channel_id=1, source_target_pairs={{0,28},{4,0},{8,4},{12,8},{16,12},{20,16},{24,20},{28,24},{1,29},{... | collective-permute-start | bytes 393224 | tf_op jit(solution)/shard_map/ppermute | solution.py:107
  337.4 32.3 %collective-permute-done.2 = f32[1,2,2,32,16,16]{3,5,0,4,2,1:T(8,128)S(1)} collective-permute-done((f32[1,2,2,32,16,16]{3,5,0,4,2,1:T(8,128)S(1)}, f32[1,2,2,32,16,16]{3,5,0,4,2,1:T(8,128)S(1)}, u32[]{:S(2)}, u32[]{:S(2)}) %collective-permute-start.2) | collective-permute-done | bytes 131104 | tf_op jit(solution)/shard_map/ppermute | solution.py:107
  384.6 89.0 %all-gather.2.cloned.1.call-done = f32[2,32,128,128]{3,2,1,0:T(8,128)} async-done(((f32[2,32,16,128]{3,2,1,0:T(8,128)}), f32[2,32,128,128]{3,2,1,0:T(8,128)}) %all-gather.2.cloned.1.call-update) | async-done | bytes 4194320 | tf_op jit(solution)/shard_map/all_gather | solution.py:128
  473.6 4.5 fusion.2
  492.2 4.4 copy.189
  496.7 5.1 all-to-all-start.3
  501.7 3.9 fusion.10
  517.5 4.4 copy.202
  521.9 27.8 %all-to-all-done.3 = f32[2,1,128,128,32]{3,4,1,0,2:T(8,128)} async-done(((f32[2,1,128,128,32]{3,4,1,0,2:T(8,128)}), f32[2,1,128,128,32]{3,4,1,0,2:T(8,128)}, u32[]{:S(2)}, u32[]{:S(2)}) %all-to-all-start.3) | async-done | bytes 4194336 | tf_op jit(solution)/shard_map/all_to_all | solution.py:143
  549.7 4.8 all-to-all-start.4
  561.9 5.1 multiply_bitcast_fusion.3
  570.7 4.9 multiply_bitcast_fusion.2
  575.6 27.2 %all-to-all-done.4 = f32[2,1,128,128,32]{3,4,1,0,2:T(8,128)} async-done(((f32[2,1,128,128,32]{3,4,1,0,2:T(8,128)}), f32[2,1,128,128,32]{3,4,1,0,2:T(8,128)}, u32[]{:S(2)}, u32[]{:S(2)}) %all-to-all-start.4) | async-done | bytes 4194336 | tf_op jit(solution)/shard_map/all_to_all | solution.py:143
  (136 shorter events, 153.7 us)
Async XLA Ops:
  7.2 248.8 %copy-start = (f32[32,128,128]{2,1,0:T(8,128)S(1)}, f32[32,128,128]{2,1,0:T(8,128)}, u32[]{:S(2)}) copy-start(f32[32,128,128]{2,1,0:T(8,128)} %param.7) | copy-start | bytes 6291460
  7.2 97.4 %reduce-scatter.2.cloned.1.call-start = ((), (), s32[]{:S(2)}) async-start(), calls=%async_computation.6 | async-start | bytes 4718592 | tf_op jit(solution)/shard_map/reduce_scatter | solution.py:122
  7.2 3.0 copy-start.7
  8.9 1.4 copy-start.5
  117.6 30.2 %all-to-all-start = ((f32[8,1,32768]{2,1,0:T(1,128)}), f32[8,1,32768]{2,1,0:T(1,128)S(1)}, u32[]{:S(2)}, u32[]{:S(2)}) async-start(f32[8,1,32768]{2,1,0:T(1,128)} %reshape.258), calls=%async_computation.1 | async-start | bytes 2097152 | tf_op jit(solution)/shard_map/all_to_all | solution.py:70
  147.9 1.0 copy-start.11
  194.9 18.7 %all-to-all-start.1 = ((f32[4,1,65536]{2,1,0:T(1,128)}), f32[4,1,65536]{2,1,0:T(1,128)}, u32[]{:S(2)}, u32[]{:S(2)}) async-start(f32[4,1,65536]{2,1,0:T(1,128)} %reshape.260), calls=%async_computation.2 | async-start | bytes 2097152 | tf_op jit(solution)/shard_map/all_to_all | solution.py:76
  251.8 17.9 %all-to-all-start.2 = ((f32[4,1,65536]{2,1,0:T(1,128)}), f32[4,1,65536]{2,1,0:T(1,128)S(1)}, u32[]{:S(2)}, u32[]{:S(2)}) async-start(f32[4,1,65536]{2,1,0:T(1,128)} %reshape.262), calls=%async_computation.3 | async-start | bytes 2097152 | tf_op jit(solution)/shard_map/all_to_all | solution.py:94
  255.3 218.3 %all-gather.2.cloned.1.call-start = ((), (), s32[]{:S(2)}) async-start(), calls=%async_computation.7 | async-start | bytes 4718592 | tf_op jit(solution)/shard_map/all_gather | solution.py:128
  289.2 2.5 copy-start.12
  295.4 3.3 copy-start.4
  297.3 17.6 %collective-permute-start = (f32[1,2,2,32,16,16]{3,5,0,4,2,1:T(8,128)S(1)}, f32[1,2,2,32,16,16]{3,5,0,4,2,1:T(8,128)S(1)}, u32[]{:S(2)}, u32[]{:S(2)}) collective-permute-start(f32[1,2,2,32,16,16]{3,5,0,4,2,1:T(8,128)S(1)} %get-tuple-element.21), channel_id=1, source_target_pairs={{0,4},{4,8},{8,12},{12,16},{16,20},{20,24},{24,28},{28,0},{1,5},{5... | collective-permute-start | bytes 393224 | tf_op jit(solution)/shard_map/ppermute | solution.py:107
  299.2 16.6 %collective-permute-start.1 = (f32[1,2,2,32,16,16]{3,5,0,4,2,1:T(8,128)S(1)}, f32[1,2,2,32,16,16]{3,5,0,4,2,1:T(8,128)S(1)}, u32[]{:S(2)}, u32[]{:S(2)}) collective-permute-start(f32[1,2,2,32,16,16]{3,5,0,4,2,1:T(8,128)S(1)} %get-tuple-element.22), channel_id=1, source_target_pairs={{0,8},{4,12},{8,16},{12,20},{16,24},{20,28},{24,0},{28,4},{1,9},{5... | collective-permute-start | bytes 393224 | tf_op jit(solution)/shard_map/ppermute | solution.py:107
  299.3 71.2 %collective-permute-start.5 = (f32[1,2,2,32,16,16]{3,5,0,4,2,1:T(8,128)S(1)}, f32[1,2,2,32,16,16]{3,5,0,4,2,1:T(8,128)S(1)}, u32[]{:S(2)}, u32[]{:S(2)}) collective-permute-start(f32[1,2,2,32,16,16]{3,5,0,4,2,1:T(8,128)S(1)} %fusion.53), channel_id=1, source_target_pairs={{0,24},{4,28},{8,0},{12,4},{16,8},{20,12},{24,16},{28,20},{1,25},{... | collective-permute-start | bytes 393224 | tf_op jit(solution)/shard_map/ppermute | solution.py:107
  303.2 66.5 %collective-permute-start.2 = (f32[1,2,2,32,16,16]{3,5,0,4,2,1:T(8,128)S(1)}, f32[1,2,2,32,16,16]{3,5,0,4,2,1:T(8,128)S(1)}, u32[]{:S(2)}, u32[]{:S(2)}) collective-permute-start(f32[1,2,2,32,16,16]{3,5,0,4,2,1:T(8,128)S(1)} %get-tuple-element.23), channel_id=1, source_target_pairs={{0,12},{4,16},{8,20},{12,24},{16,28},{20,0},{24,4},{28,8},{1,13},{... | collective-permute-start | bytes 393224 | tf_op jit(solution)/shard_map/ppermute | solution.py:107
  303.2 67.2 %collective-permute-start.3 = (f32[1,2,2,32,16,16]{3,5,0,4,2,1:T(8,128)S(1)}, f32[1,2,2,32,16,16]{3,5,0,4,2,1:T(8,128)S(1)}, u32[]{:S(2)}, u32[]{:S(2)}) collective-permute-start(f32[1,2,2,32,16,16]{3,5,0,4,2,1:T(8,128)S(1)} %get-tuple-element.24), channel_id=1, source_target_pairs={{0,16},{4,20},{8,24},{12,28},{16,0},{20,4},{24,8},{28,12},{1,17},{... | collective-permute-start | bytes 393224 | tf_op jit(solution)/shard_map/ppermute | solution.py:107
  315.0 55.5 %collective-permute-start.4 = (f32[1,2,2,32,16,16]{3,5,0,4,2,1:T(8,128)S(1)}, f32[1,2,2,32,16,16]{3,5,0,4,2,1:T(8,128)S(1)}, u32[]{:S(2)}, u32[]{:S(2)}) collective-permute-start(f32[1,2,2,32,16,16]{3,5,0,4,2,1:T(8,128)S(1)} %get-tuple-element.25), channel_id=1, source_target_pairs={{0,20},{4,24},{8,28},{12,0},{16,4},{20,8},{24,12},{28,16},{1,21},{... | collective-permute-start | bytes 393224 | tf_op jit(solution)/shard_map/ppermute | solution.py:107
  315.8 54.8 %collective-permute-start.6 = (f32[1,2,2,32,16,16]{3,5,0,4,2,1:T(8,128)S(1)}, f32[1,2,2,32,16,16]{3,5,0,4,2,1:T(8,128)S(1)}, u32[]{:S(2)}, u32[]{:S(2)}) collective-permute-start(f32[1,2,2,32,16,16]{3,5,0,4,2,1:T(8,128)S(1)} %get-tuple-element.20), channel_id=1, source_target_pairs={{0,28},{4,0},{8,4},{12,8},{16,12},{20,16},{24,20},{28,24},{1,29},{... | collective-permute-start | bytes 393224 | tf_op jit(solution)/shard_map/ppermute | solution.py:107
  377.0 1.0 copy-start.10
  381.4 92.3 %copy-start.6 = (f32[32,128,128]{2,1,0:T(8,128)S(1)}, f32[32,128,128]{2,1,0:T(8,128)}, u32[]{:S(2)}) copy-start(f32[32,128,128]{2,1,0:T(8,128)} %copy-done.5) | copy-start | bytes 6291460
  478.2 2.2 copy-start.2
  496.7 53.1 %all-to-all-start.3 = ((f32[2,1,128,128,32]{3,4,1,0,2:T(8,128)}), f32[2,1,128,128,32]{3,4,1,0,2:T(8,128)}, u32[]{:S(2)}, u32[]{:S(2)}) async-start(f32[2,1,128,128,32]{3,4,1,0,2:T(8,128)} %copy.189), calls=%async_computation.4 | async-start | bytes 8388608 | tf_op jit(solution)/shard_map/all_to_all | solution.py:143
  501.7 3.9 copy-start.3
  549.7 53.1 %all-to-all-start.4 = ((f32[2,1,128,128,32]{3,4,1,0,2:T(8,128)}), f32[2,1,128,128,32]{3,4,1,0,2:T(8,128)}, u32[]{:S(2)}, u32[]{:S(2)}) async-start(f32[2,1,128,128,32]{3,4,1,0,2:T(8,128)} %copy.202), calls=%async_computation.5 | async-start | bytes 8388608 | tf_op jit(solution)/shard_map/all_to_all | solution.py:143
  617.6 3.6 copy-start.8
  617.6 3.6 copy-start.9
  622.2 3.6 copy-start.1
Sparse Core Ops, SparseCore 0:
  13.1 91.3 reduce-scatter.1
  380.8 92.7 all-gather.1
